TPU v7x, 32 devices: a whole 2x2x4 slice. The times are simulated.
32 devices in a mesh: dp: 8 (over z, x), mp: 4 (over y, core).
Axes of the slice: x: 2, y: 2, z: 4, core: 2. Of those that a mesh axis runs over, the one named last changes fastest.
Arguments:
- patches: bfloat16 [4096, 2048], P('dp'), may hold values from -6 to 6
- cotangent: bfloat16 [4096, 8192], P('dp', 'mp'), may hold values from -0.09375 to 0.09375
- weight: float32 [2048, 8192], P('dp', 'mp'), may hold values from -0.125 to 0.125
- accum: float32 [2048, 8192], P('dp', 'mp'), may hold values from 0.1 to 4
Outputs:
- new_weight: float32 [2048, 8192], P(('dp', 'mp'))
- new_accum: float32 [2048, 8192], P(('dp', 'mp'))
- weight_copy: bfloat16 [2048, 8192], P(None, 'mp')
All inputs are finite; a program needn't handle non-finite values.
Results may differ from a plain program's by a relative error of at most 0.001.
Values may be sent and summed in bfloat16 or wider, within the bound.
A program may use at most 192 MiB of HBM per device.

v0:
```python
import jax
import jax.numpy as jnp
from jax import lax
from jax.sharding import PartitionSpec as P

learning_rate = 0.02


def adagrad(accum, weight, grad):
    summed = accum + grad * grad
    return (summed, weight - learning_rate * grad * lax.rsqrt(summed))


def shards(patches, cotangent, weight, accum):
    patch_block = lax.all_to_all(patches, "dp", split_axis=1, concat_axis=0, tiled=True)
    grad_block = jnp.einsum(
        "tr,tf->rf",
        patch_block,
        lax.all_gather(cotangent, "dp", axis=0, tiled=True),
        preferred_element_type=jnp.float32,
    )
    accum_block, weight_block = adagrad(accum, weight, grad_block)
    weight_copy = lax.all_gather(weight_block.astype(jnp.bfloat16), "dp", axis=0, tiled=True)
    new_accum, new_weight = (
        lax.all_to_all(accum_block, "mp", split_axis=0, concat_axis=1, tiled=True),
        lax.all_to_all(weight_block, "mp", split_axis=0, concat_axis=1, tiled=True),
    )
    return (new_weight, new_accum, weight_copy)


def solution(mesh):
    return jax.shard_map(
        shards,
        mesh=mesh,
        in_specs=(P("dp", None), P("dp", "mp"), P("dp", "mp"), P("dp", "mp")),
        out_specs=(P(("dp", "mp"), None), P(("dp", "mp"), None), P(None, "mp")),
        check_vma=False,
    )
```

profile of v0, /device:TPU:0, one launch (start us, length us, event | category | flops | bytes accessed | tf_op | source)
XLA Modules:
  0.0 430.2 jit_solution(2336489553796141500)
XLA Ops:
  7.2 0.0 all-gather.3.cloned.1.call-start
  7.2 0.7 all-gather.3.cloned.1.call-update
  7.9 0.0 all-gather.5.cloned.1.call-start
  7.9 2.9 copy.11
  10.8 107.2 %all_to_all.57 = bf16[512,8,256]{0,2,1:T(8,128)(2,1)} all-to-all(bf16[512,8,256]{0,2,1:T(8,128)(2,1)S(1)} %bitcast.18), channel_id=1, replica_groups=mesh['dp'=8,'mp'=4] {'dp'}, dimensions={1} | all-to-all | bytes 4194304 | tf_op jit(solution)/shard_map/all_to_all | solution.py:15
  118.0 2.8 copy.12
  120.9 158.3 %all-gather.3.cloned.1.call-done = bf16[4096,2048]{1,0:T(8,128)(2,1)} async-done(((bf16[512,2048]{1,0:T(8,128)(2,1)}), bf16[4096,2048]{1,0:T(8,128)(2,1)}) %all-gather.3.cloned.1.call-update) | async-done | bytes 16777232 | tf_op jit(solution)/shard_map/all_gather | solution.py:19
  279.1 12.9 %fusion = (bf16[256,2048]{1,0:T(8,128)(2,1)}, f32[256,2048]{1,0:T(8,128)}, f32[256,2048]{1,0:T(8,128)}) fusion(f32[256,2048]{1,0:T(8,128)} %param.6, f32[256,2048]{1,0:T(8,128)} %param.7, bf16[4096,256]{1,0:T(8,128)(2,1)S(1)} %bitcast.13, bf16[4096,2048]{1,0:T(8,128)(2,1)} %all-gather.3.cloned.1.call-done), kind=kOutput, calls=%fused_computation.2 | convolution fusion | flops 4298113024 | bytes 28311552 | tf_op jit(solution)/shard_map/tr,tf->rf/dot_general | solution.py:16
  292.0 0.0 all-gather.5.cloned.1.call-update
  292.1 30.2 %all_to_all.58 = f32[4,64,2048]{2,1,0:T(8,128)} all-to-all(f32[4,64,2048]{2,1,0:T(8,128)} %bitcast.14), channel_id=1, replica_groups=mesh['dp'=8,'mp'=4] {'mp'}, dimensions={0} | all-to-all | bytes 4194304 | tf_op jit(solution)/shard_map/all_to_all | solution.py:26
  322.2 3.6 all-to-all-start.2
  325.8 3.1 copy.15
  329.0 22.5 %all-to-all-done.2 = f32[4,64,2048]{2,1,0:T(8,128)S(1)} async-done(((f32[4,64,2048]{2,1,0:T(8,128)}), f32[4,64,2048]{2,1,0:T(8,128)S(1)}, u32[]{:S(2)}, u32[]{:S(2)}) %all-to-all-start.2) | async-done | bytes 2097184 | tf_op jit(solution)/shard_map/all_to_all | solution.py:25
  351.5 1.5 copy.16
  352.9 61.9 %all-gather.5.cloned.1.call-done = bf16[2048,2048]{1,0:T(8,128)(2,1)} async-done(((bf16[256,2048]{1,0:T(8,128)(2,1)}), bf16[2048,2048]{1,0:T(8,128)(2,1)}) %all-gather.5.cloned.1.call-update) | async-done | bytes 8388624 | tf_op jit(solution)/shard_map/all_gather | solution.py:23
  414.9 8.4 %copy.18 = bf16[2048,2048]{1,0:T(8,128)(2,1)} copy(bf16[2048,2048]{1,0:T(8,128)(2,1)} %all-gather.5.cloned.1.call-done) | data formatting | bytes 16777216
Async XLA Ops:
  7.2 272.0 %all-gather.3.cloned.1.call-start = ((), (), s32[]{:S(2)}) async-start(), calls=%async_computation.3 | async-start | bytes 18874368 | tf_op jit(solution)/shard_map/all_gather | solution.py:19
  7.9 407.0 %all-gather.5.cloned.1.call-start = ((), (), s32[]{:S(2)}) async-start(), calls=%async_computation.4 | async-start | bytes 9437184 | tf_op jit(solution)/shard_map/all_gather | solution.py:23
  322.2 29.3 %all-to-all-start.2 = ((f32[4,64,2048]{2,1,0:T(8,128)}), f32[4,64,2048]{2,1,0:T(8,128)S(1)}, u32[]{:S(2)}, u32[]{:S(2)}) async-start(f32[4,64,2048]{2,1,0:T(8,128)} %bitcast.5), calls=%async_computation.2 | async-start | bytes 4194304 | tf_op jit(solution)/shard_map/all_to_all | solution.py:25
Sparse Core Ops, SparseCore 0:
  10.1 268.9 all-gather.2
  292.2 122.6 all-gather.4
where the time goes:
time: 431 us; the launch traced here: 430 us
  waiting for transfers between devices  243 us (56%)
  blocking collectives  137 us (32%)
  local copies, waits for them, and re-layouts  18.8 us (4%)
  between operations  14.1 us (3%)
  matrix products  12.9 us (3%)
    all_gather x1, waiting for transfers between devices, shards(): lax.all_gather(cotangent, 'dp', axis=0, tiled=True)  158 us
    all_to_all x1, blocking collectives, shards(): lax.all_to_all(patches, 'dp', split_axis=1, concat_axis=0, tiled=True)  107 us
    all_gather x1, waiting for transfers between devices, shards(): lax.all_gather(weight_block.astype(jnp.bfloat16), 'dp', axis=0, tiled=True)  61.9 us
    all_to_all x1, blocking collectives, shards(): lax.all_to_all(weight_block, 'mp', split_axis=0, concat_axis=1, tiled=True)  30.2 us
    all_to_all x1, waiting for transfers between devices, shards(): lax.all_to_all(accum_block, 'mp', split_axis=0, concat_axis=1, tiled=True)  22.5 us
    dot_general x1, matrix products, shards(): jnp.einsum('tr,tf->rf', patch_block, lax.all_gather(cotangent, 'dp', axis...  12.9 us
    unnamed x2, local copies, waits for them, and re-layouts  11.3 us
  transfers between devices with their start and end apart: 3, of which 3 were waited for; matrix products, arithmetic and copies ran while one was open for 2% of the time, Pallas kernels for 0%

commit v1 on v0

--- a/solution.py
+++ b/solution.py
@@ -22,7 +22,12 @@
     accum_block, weight_block = adagrad(accum, weight, grad_block)
     weight_copy = lax.all_gather(weight_block.astype(jnp.bfloat16), "dp", axis=0, tiled=True)
     new_accum, new_weight = (
-        lax.all_to_all(accum_block, "mp", split_axis=0, concat_axis=1, tiled=True),
+        jnp.concatenate(
+            lax.all_to_all(
+                jnp.stack(jnp.split(accum_block, lax.axis_size("mp"), axis=0)), "mp", 0, 0
+            ),
+            axis=1,
+        ),
         lax.all_to_all(weight_block, "mp", split_axis=0, concat_axis=1, tiled=True),
     )
     return (new_weight, new_accum, weight_copy)

time: 431 us -> 431 us (level)
  blocking collectives: 137 us -> 107 us
  waiting for transfers between devices: 243 us -> 267 us
  starting transfers between devices: 3.69 us -> 8.31 us
    all_to_all x1 -> x0, blocking collectives: 30.2 us -> none  [shards(): lax.all_to_all(weight_block, 'mp', split_axis=0, concat_axis=1, tiled=True)]
    all_to_all x1 -> x2, waiting for transfers between devices: 22.5 us -> 46.5 us  [the longest x1 24 us: shards(): lax.all_to_all(weight_block, 'mp', split_axis=0, concat_axis=1, tiled=True)]
    all_to_all x1 -> x2, starting transfers between devices: 3.61 us -> 8.23 us  [the longest x1 4.62 us: shards(): lax.all_to_all(weight_block, 'mp', split_axis=0, concat_axis=1, tiled=True)]
    unnamed x2 -> x4, local copies, waits for them, and re-layouts: 11.3 us -> 11.3 us
  transfers between devices with their start and end apart: 3 -> 4, of which waited for: 3 -> 4; matrix products, arithmetic and copies ran while one was open for 2% -> 3% of each run, Pallas kernels for 0% -> 0%
where the time goes in v1:
time: 431 us; the launch traced here: 430 us
  waiting for transfers between devices  267 us (62%)
  blocking collectives  107 us (25%)
  local copies, waits for them, and re-layouts  19 us (4%)
  between operations  14.1 us (3%)
  matrix products  12.9 us (3%)
  starting transfers between devices  8.31 us (2%)
    all_gather x1, waiting for transfers between devices, shards(): lax.all_gather(cotangent, 'dp', axis=0, tiled=True)  158 us
    all_to_all x1, blocking collectives, shards(): lax.all_to_all(patches, 'dp', split_axis=1, concat_axis=0, tiled=True)  107 us
    all_gather x1, waiting for transfers between devices, shards(): lax.all_gather(weight_block.astype(jnp.bfloat16), 'dp', axis=0, tiled=True)  61.7 us
    all_to_all x1, waiting for transfers between devices, shards(): lax.all_to_all(weight_block, 'mp', split_axis=0, concat_axis=1, tiled=True)  24 us
    all_to_all x1, waiting for transfers between devices, shards(): lax.all_to_all(jnp.stack(jnp.split(accum_block, lax.axis_size('mp'), axis...  22.5 us
    dot_general x1, matrix products, shards(): jnp.einsum('tr,tf->rf', patch_block, lax.all_gather(cotangent, 'dp', axis...  12.9 us
    unnamed x4, local copies, waits for them, and re-layouts  11.3 us
  transfers between devices with their start and end apart: 4, of which 4 were waited for; matrix products, arithmetic and copies ran while one was open for 3% of the time, Pallas kernels for 0%

profile of v1, /device:TPU:0, one launch (start us, length us, event | category | flops | bytes accessed | tf_op | source)
XLA Modules:
  0.0 430.2 jit_solution(9312415228654659077)
XLA Ops:
  7.2 0.0 all-gather.3.cloned.1.call-start
  7.2 0.7 all-gather.3.cloned.1.call-update
  7.9 0.0 all-gather.5.cloned.1.call-start
  7.9 2.9 copy.10
  10.8 107.2 %all_to_all.43 = bf16[512,8,256]{0,2,1:T(8,128)(2,1)} all-to-all(bf16[512,8,256]{0,2,1:T(8,128)(2,1)S(1)} %bitcast.24), channel_id=1, replica_groups=mesh['dp'=8,'mp'=4] {'dp'}, dimensions={1} | all-to-all | bytes 4194304 | tf_op jit(solution)/shard_map/all_to_all | solution.py:15
  118.0 2.8 copy.11
  120.9 158.3 %all-gather.3.cloned.1.call-done = bf16[4096,2048]{1,0:T(8,128)(2,1)} async-done(((bf16[512,2048]{1,0:T(8,128)(2,1)}), bf16[4096,2048]{1,0:T(8,128)(2,1)}) %all-gather.3.cloned.1.call-update) | async-done | bytes 16777232 | tf_op jit(solution)/shard_map/all_gather | solution.py:19
  279.1 12.9 %fusion = (bf16[256,2048]{1,0:T(8,128)(2,1)}, f32[256,2048]{1,0:T(8,128)}, f32[256,2048]{1,0:T(8,128)}) fusion(f32[256,2048]{1,0:T(8,128)} %param.6, f32[256,2048]{1,0:T(8,128)} %param.7, bf16[4096,256]{1,0:T(8,128)(2,1)S(1)} %bitcast.20, bf16[4096,2048]{1,0:T(8,128)(2,1)} %all-gather.3.cloned.1.call-done), kind=kOutput, calls=%fused_computation.7 | convolution fusion | flops 4298113024 | bytes 28311552 | tf_op jit(solution)/shard_map/tr,tf->rf/dot_general | solution.py:16
  292.0 0.0 all-gather.5.cloned.1.call-update
  292.1 0.0 copy-start
  292.1 4.6 %all-to-all-start.1 = ((f32[4,64,2048]{2,1,0:T(8,128)}), f32[4,64,2048]{2,1,0:T(8,128)}, u32[]{:S(2)}, u32[]{:S(2)}) async-start(f32[4,64,2048]{2,1,0:T(8,128)} %bitcast.21), calls=%async_computation.1 | async-start | bytes 4194304 | tf_op jit(solution)/shard_map/all_to_all | solution.py:31
  296.7 0.0 copy-done
  296.7 0.2 slice_bitcast_fusion.3
  296.9 1.5 pad_maximum_fusion
  298.4 24.0 %all-to-all-done.1 = f32[4,64,2048]{2,1,0:T(8,128)} async-done(((f32[4,64,2048]{2,1,0:T(8,128)}), f32[4,64,2048]{2,1,0:T(8,128)}, u32[]{:S(2)}, u32[]{:S(2)}) %all-to-all-start.1) | async-done | bytes 2097184 | tf_op jit(solution)/shard_map/all_to_all | solution.py:31
  322.4 3.6 all-to-all-start.2
  326.1 3.1 copy.14
  329.2 22.5 %all-to-all-done.2 = f32[4,64,2048]{2,1,0:T(8,128)S(1)} async-done(((f32[4,64,2048]{2,1,0:T(8,128)}), f32[4,64,2048]{2,1,0:T(8,128)S(1)}, u32[]{:S(2)}, u32[]{:S(2)}) %all-to-all-start.2) | async-done | bytes 2097184 | tf_op jit(solution)/shard_map/all_to_all | solution.py:26
  351.7 1.5 copy.15
  353.1 61.7 %all-gather.5.cloned.1.call-done = bf16[2048,2048]{1,0:T(8,128)(2,1)} async-done(((bf16[256,2048]{1,0:T(8,128)(2,1)}), bf16[2048,2048]{1,0:T(8,128)(2,1)}) %all-gather.5.cloned.1.call-update) | async-done | bytes 8388624 | tf_op jit(solution)/shard_map/all_gather | solution.py:23
  414.9 8.4 %copy.17 = bf16[2048,2048]{1,0:T(8,128)(2,1)} copy(bf16[2048,2048]{1,0:T(8,128)(2,1)} %all-gather.5.cloned.1.call-done) | data formatting | bytes 16777216
Async XLA Ops:
  7.2 272.0 %all-gather.3.cloned.1.call-start = ((), (), s32[]{:S(2)}) async-start(), calls=%async_computation.3 | async-start | bytes 18874368 | tf_op jit(solution)/shard_map/all_gather | solution.py:19
  7.9 407.0 %all-gather.5.cloned.1.call-start = ((), (), s32[]{:S(2)}) async-start(), calls=%async_computation.4 | async-start | bytes 9437184 | tf_op jit(solution)/shard_map/all_gather | solution.py:23
  292.1 4.6 %copy-start = (f32[256,2048]{1,0:T(8,128)S(1)}, f32[256,2048]{1,0:T(8,128)}, u32[]{:S(2)}) copy-start(f32[256,2048]{1,0:T(8,128)} %get-tuple-element.5) | copy-start | bytes 6291460
  292.1 30.4 %all-to-all-start.1 = ((f32[4,64,2048]{2,1,0:T(8,128)}), f32[4,64,2048]{2,1,0:T(8,128)}, u32[]{:S(2)}, u32[]{:S(2)}) async-start(f32[4,64,2048]{2,1,0:T(8,128)} %bitcast.21), calls=%async_computation.1 | async-start | bytes 4194304 | tf_op jit(solution)/shard_map/all_to_all | solution.py:31
  322.4 29.3 %all-to-all-start.2 = ((f32[4,64,2048]{2,1,0:T(8,128)}), f32[4,64,2048]{2,1,0:T(8,128)S(1)}, u32[]{:S(2)}, u32[]{:S(2)}) async-start(f32[4,64,2048]{2,1,0:T(8,128)} %pad_maximum_fusion), calls=%async_computation.2 | async-start | bytes 4194304 | tf_op jit(solution)/shard_map/all_to_all | solution.py:26
Sparse Core Ops, SparseCore 0:
  10.1 268.9 all-gather.2
  292.2 122.6 all-gather.4

commit v2 on v0

--- a/solution.py
+++ b/solution.py
@@ -13,12 +13,38 @@
 
 def shards(patches, cotangent, weight, accum):
     patch_block = lax.all_to_all(patches, "dp", split_axis=1, concat_axis=0, tiled=True)
-    grad_block = jnp.einsum(
+    devices, index, rows = (lax.axis_size("dp"), lax.axis_index("dp"), cotangent.shape[0])
+    right = [(i, (i + 1) % devices) for i in range(devices)]
+    downward = [(i, (i - 1) % devices) for i in range(devices)]
+    half = devices // 2
+    from_left = from_right = cotangent
+    total = jnp.einsum(
         "tr,tf->rf",
-        patch_block,
-        lax.all_gather(cotangent, "dp", axis=0, tiled=True),
+        lax.dynamic_slice_in_dim(patch_block, index * rows, cotangent.shape[0], axis=0),
+        cotangent,
         preferred_element_type=jnp.float32,
     )
+    for hop in range(1, half + 1):
+        from_left = lax.ppermute(from_left, "dp", right)
+        if hop < devices - half:
+            from_right = lax.ppermute(from_right, "dp", downward)
+            total = total + jnp.einsum(
+                "tr,tf->rf",
+                lax.dynamic_slice_in_dim(
+                    patch_block, (index + hop) % devices * rows, from_right.shape[0], axis=0
+                ),
+                from_right,
+                preferred_element_type=jnp.float32,
+            )
+        total = total + jnp.einsum(
+            "tr,tf->rf",
+            lax.dynamic_slice_in_dim(
+                patch_block, (index - hop) % devices * rows, from_left.shape[0], axis=0
+            ),
+            from_left,
+            preferred_element_type=jnp.float32,
+        )
+    grad_block = total
     accum_block, weight_block = adagrad(accum, weight, grad_block)
     weight_copy = lax.all_gather(weight_block.astype(jnp.bfloat16), "dp", axis=0, tiled=True)
     new_accum, new_weight = (

time: 431 us -> 499 us (1.16)
  waiting for transfers between devices: 243 us -> 392 us
  blocking collectives: 137 us -> 28.9 us
  starting transfers between devices: 3.69 us -> 26.4 us
    ppermute x0 -> x7, waiting for transfers between devices: none -> 302 us  [the longest x4 182 us: shards(): from_left = lax.ppermute(from_left, 'dp', right)]
    all_gather x1 -> x0, waiting for transfers between devices: 158 us -> none  [shards(): lax.all_gather(cotangent, 'dp', axis=0, tiled=True)]
    all_to_all x1 -> x0, blocking collectives: 107 us -> none  [shards(): lax.all_to_all(patches, 'dp', split_axis=1, concat_axis=0, tiled=True)]
    ppermute x0 -> x7, starting transfers between devices: none -> 17.9 us  [the longest x4 10.1 us: shards(): from_left = lax.ppermute(from_left, 'dp', right)]
    dot_general x1 -> x8, matrix products: 12.9 us -> 17.8 us  [the longest x4 9.75 us: shards(): jnp.einsum('tr,tf->rf', lax.dynamic_slice_in_dim(patch_block, (index - ho...]
    unnamed x2 -> x8, local copies, waits for them, and re-layouts: 11.3 us -> 12.4 us
  transfers between devices with their start and end apart: 3 -> 10, of which waited for: 3 -> 7; matrix products, arithmetic and copies ran while one was open for 2% -> 5% of each run, Pallas kernels for 0% -> 0%
where the time goes in v2:
time: 499 us; the launch traced here: 498 us
  waiting for transfers between devices  392 us (79%)
  blocking collectives  28.9 us (6%)
  starting transfers between devices  26.4 us (5%)
  local copies, waits for them, and re-layouts  19.4 us (4%)
  matrix products  17.8 us (4%)
  between operations  14.1 us (3%)
    ppermute x4, waiting for transfers between devices, shards(): from_left = lax.ppermute(from_left, 'dp', right)  182 us
    ppermute x3, waiting for transfers between devices, shards(): from_right = lax.ppermute(from_right, 'dp', downward)  121 us
    all_gather x1, waiting for transfers between devices, shards(): lax.all_gather(weight_block.astype(jnp.bfloat16), 'dp', axis=0, tiled=True)  63.7 us
    all_to_all x1, blocking collectives, shards(): lax.all_to_all(weight_block, 'mp', split_axis=0, concat_axis=1, tiled=True)  28.9 us
    all_to_all x1, waiting for transfers between devices, shards(): lax.all_to_all(accum_block, 'mp', split_axis=0, concat_axis=1, tiled=True)  22.5 us
    unnamed x8, local copies, waits for them, and re-layouts  12.4 us
    ppermute x4, starting transfers between devices, shards(): from_left = lax.ppermute(from_left, 'dp', right)  10.1 us
  transfers between devices with their start and end apart: 10, of which 7 were waited for; matrix products, arithmetic and copies ran while one was open for 5% of the time, Pallas kernels for 0%

profile of v2, /device:TPU:0, one launch (start us, length us, event | category | flops | bytes accessed | tf_op | source)
XLA Modules:
  0.0 498.4 jit_solution(15570328939333143267)
XLA Ops:
  7.2 3.0 collective-permute-start.1
  10.2 3.1 collective-permute-start
  13.3 87.0 %collective-permute-done.1 = bf16[512,2048]{1,0:T(8,128)(2,1)} collective-permute-done((bf16[512,2048]{1,0:T(8,128)(2,1)}, bf16[512,2048]{1,0:T(8,128)(2,1)}, u32[]{:S(2)}, u32[]{:S(2)}) %collective-permute-start.1) | collective-permute-done | bytes 2097184 | tf_op jit(solution)/shard_map/ppermute | solution.py:28
  100.3 2.5 collective-permute-start.3
  102.8 3.9 copy.11
  106.7 4.9 all-to-all-start
  111.6 0.0 all-gather.2.cloned.1.call-start
  111.6 0.0 collective-permute-done
  111.7 4.7 collective-permute-start.2
  116.4 94.6 %collective-permute-done.3 = bf16[512,2048]{1,0:T(8,128)(2,1)} collective-permute-done((bf16[512,2048]{1,0:T(8,128)(2,1)}, bf16[512,2048]{1,0:T(8,128)(2,1)}, u32[]{:S(2)}, u32[]{:S(2)}) %collective-permute-start.3) | collective-permute-done | bytes 2097184 | tf_op jit(solution)/shard_map/ppermute | solution.py:28
  210.9 2.5 collective-permute-start.5
  213.4 3.1 all-to-all-done
  216.6 2.4 copy.12
  218.9 44.4 %collective-permute-done.2 = bf16[512,2048]{1,0:T(8,128)(2,1)} collective-permute-done((bf16[512,2048]{1,0:T(8,128)(2,1)}, bf16[512,2048]{1,0:T(8,128)(2,1)}, u32[]{:S(2)}, u32[]{:S(2)}) %collective-permute-start.2) | collective-permute-done | bytes 2097184 | tf_op jit(solution)/shard_map/ppermute | solution.py:30
  263.3 0.0 collective-permute-start.4
  263.3 0.0 copy-start
  263.3 2.5 fusion.11
  265.8 0.0 collective-permute-done.5
  265.9 2.1 collective-permute-start.6
  267.9 0.0 copy-done
  267.9 2.3 convolution_add_fusion.4
  270.3 2.3 convolution_add_fusion.3
  272.6 2.3 fusion.6
  275.0 2.4 fusion.1
  277.3 2.3 fusion.3
  279.6 0.0 copy-start.1
  279.7 0.0 copy-start.2
  279.7 76.3 %collective-permute-done.4 = bf16[512,2048]{1,0:T(8,128)(2,1)S(1)} collective-permute-done((bf16[512,2048]{1,0:T(8,128)(2,1)}, bf16[512,2048]{1,0:T(8,128)(2,1)S(1)}, u32[]{:S(2)}, u32[]{:S(2)}) %collective-permute-start.4) | collective-permute-done | bytes 2097184 | tf_op jit(solution)/shard_map/ppermute | solution.py:30
  356.0 0.8 fusion
  356.8 0.0 collective-permute-done.6
  356.8 0.0 copy-done.1
  356.8 0.0 copy-done.2
  356.9 2.7 fusion.21
  359.6 0.0 all-gather.2.cloned.1.call-update
  359.6 28.9 %all_to_all.57 = f32[4,64,2048]{2,1,0:T(8,128)} all-to-all(f32[4,64,2048]{2,1,0:T(8,128)S(1)} %bitcast.32), channel_id=1, replica_groups=mesh['dp'=8,'mp'=4] {'mp'}, dimensions={0} | all-to-all | bytes 4194304 | tf_op jit(solution)/shard_map/all_to_all | solution.py:52
  388.6 3.6 all-to-all-start.2
  392.2 3.2 copy.15
  395.3 22.5 %all-to-all-done.2 = f32[4,64,2048]{2,1,0:T(8,128)S(1)} async-done(((f32[4,64,2048]{2,1,0:T(8,128)}), f32[4,64,2048]{2,1,0:T(8,128)S(1)}, u32[]{:S(2)}, u32[]{:S(2)}) %all-to-all-start.2) | async-done | bytes 2097184 | tf_op jit(solution)/shard_map/all_to_all | solution.py:51
  417.8 1.5 copy.16
  419.4 63.7 %all-gather.2.cloned.1.call-done = bf16[2048,2048]{1,0:T(8,128)(2,1)} async-done(((bf16[256,2048]{1,0:T(8,128)(2,1)}), bf16[2048,2048]{1,0:T(8,128)(2,1)}) %all-gather.2.cloned.1.call-update) | async-done | bytes 8388624 | tf_op jit(solution)/shard_map/all_gather | solution.py:49
  483.1 8.4 %copy.18 = bf16[2048,2048]{1,0:T(8,128)(2,1)} copy(bf16[2048,2048]{1,0:T(8,128)(2,1)} %all-gather.2.cloned.1.call-done) | data formatting | bytes 16777216
Async XLA Ops:
  7.2 93.2 %collective-permute-start.1 = (bf16[512,2048]{1,0:T(8,128)(2,1)}, bf16[512,2048]{1,0:T(8,128)(2,1)}, u32[]{:S(2)}, u32[]{:S(2)}) collective-permute-start(bf16[512,2048]{1,0:T(8,128)(2,1)} %param.5), channel_id=1, source_target_pairs={{0,4},{4,8},{8,12},{12,16},{16,20},{20,24},{24,28},{28,0},{1,5},{5... | collective-permute-start | bytes 6291464 | tf_op jit(solution)/shard_map/ppermute | solution.py:28
  10.2 101.5 %collective-permute-start = (bf16[512,2048]{1,0:T(8,128)(2,1)}, bf16[512,2048]{1,0:T(8,128)(2,1)}, u32[]{:S(2)}, u32[]{:S(2)}) collective-permute-start(bf16[512,2048]{1,0:T(8,128)(2,1)} %param.5), channel_id=1, source_target_pairs={{0,28},{4,0},{8,4},{12,8},{16,12},{20,16},{24,20},{28,24},{1,29},{... | collective-permute-start | bytes 6291464 | tf_op jit(solution)/shard_map/ppermute | solution.py:30
  100.3 110.6 %collective-permute-start.3 = (bf16[512,2048]{1,0:T(8,128)(2,1)}, bf16[512,2048]{1,0:T(8,128)(2,1)}, u32[]{:S(2)}, u32[]{:S(2)}) collective-permute-start(bf16[512,2048]{1,0:T(8,128)(2,1)} %collective-permute-done.1), channel_id=1, source_target_pairs={{0,4},{4,8},{8,12},{12,16},{16,20},{20,24},{24,28},{28,0},{1,5},{5... | collective-permute-start | bytes 6291464 | tf_op jit(solution)/shard_map/ppermute | solution.py:28
  106.7 109.8 %all-to-all-start = ((bf16[512,8,256]{0,2,1:T(8,128)(2,1)}), bf16[512,8,256]{0,2,1:T(8,128)(2,1)S(1)}, u32[]{:S(2)}, u32[]{:S(2)}) async-start(bf16[512,8,256]{0,2,1:T(8,128)(2,1)} %bitcast.20), calls=%async_computation | async-start | bytes 4194304 | tf_op jit(solution)/shard_map/all_to_all | solution.py:15
  111.6 371.5 %all-gather.2.cloned.1.call-start = ((), (), s32[]{:S(2)}) async-start(), calls=%async_computation.3 | async-start | bytes 9437184 | tf_op jit(solution)/shard_map/all_gather | solution.py:49
  111.7 151.6 %collective-permute-start.2 = (bf16[512,2048]{1,0:T(8,128)(2,1)}, bf16[512,2048]{1,0:T(8,128)(2,1)}, u32[]{:S(2)}, u32[]{:S(2)}) collective-permute-start(bf16[512,2048]{1,0:T(8,128)(2,1)} %collective-permute-done), channel_id=1, source_target_pairs={{0,28},{4,0},{8,4},{12,8},{16,12},{20,16},{24,20},{28,24},{1,29},{... | collective-permute-start | bytes 6291464 | tf_op jit(solution)/shard_map/ppermute | solution.py:30
  210.9 54.9 %collective-permute-start.5 = (bf16[512,2048]{1,0:T(8,128)(2,1)}, bf16[512,2048]{1,0:T(8,128)(2,1)}, u32[]{:S(2)}, u32[]{:S(2)}) collective-permute-start(bf16[512,2048]{1,0:T(8,128)(2,1)} %collective-permute-done.3), channel_id=1, source_target_pairs={{0,4},{4,8},{8,12},{12,16},{16,20},{20,24},{24,28},{28,0},{1,5},{5... | collective-permute-start | bytes 6291464 | tf_op jit(solution)/shard_map/ppermute | solution.py:28
  263.3 92.7 %collective-permute-start.4 = (bf16[512,2048]{1,0:T(8,128)(2,1)}, bf16[512,2048]{1,0:T(8,128)(2,1)S(1)}, u32[]{:S(2)}, u32[]{:S(2)}) collective-permute-start(bf16[512,2048]{1,0:T(8,128)(2,1)} %collective-permute-done.2), channel_id=1, source_target_pairs={{0,28},{4,0},{8,4},{12,8},{16,12},{20,16},{24,20},{28,24},{1,29},{... | collective-permute-start | bytes 6291464 | tf_op jit(solution)/shard_map/ppermute | solution.py:30
  263.3 4.6 copy-start
  265.9 91.0 %collective-permute-start.6 = (bf16[512,2048]{1,0:T(8,128)(2,1)}, bf16[512,2048]{1,0:T(8,128)(2,1)S(1)}, u32[]{:S(2)}, u32[]{:S(2)}) collective-permute-start(bf16[512,2048]{1,0:T(8,128)(2,1)} %collective-permute-done.5), channel_id=1, source_target_pairs={{0,4},{4,8},{8,12},{12,16},{16,20},{20,24},{24,28},{28,0},{1,5},{5... | collective-permute-start | bytes 6291464 | tf_op jit(solution)/shard_map/ppermute | solution.py:28
  279.6 77.2 %copy-start.1 = (f32[256,2048]{1,0:T(8,128)S(1)}, f32[256,2048]{1,0:T(8,128)}, u32[]{:S(2)}) copy-start(f32[256,2048]{1,0:T(8,128)} %param.6) | copy-start | bytes 6291460
  279.7 77.2 %copy-start.2 = (f32[256,2048]{1,0:T(8,128)S(1)}, f32[256,2048]{1,0:T(8,128)}, u32[]{:S(2)}) copy-start(f32[256,2048]{1,0:T(8,128)} %param.7) | copy-start | bytes 6291460
  388.6 29.3 %all-to-all-start.2 = ((f32[4,64,2048]{2,1,0:T(8,128)}), f32[4,64,2048]{2,1,0:T(8,128)S(1)}, u32[]{:S(2)}, u32[]{:S(2)}) async-start(f32[4,64,2048]{2,1,0:T(8,128)} %bitcast.31), calls=%async_computation.2 | async-start | bytes 4194304 | tf_op jit(solution)/shard_map/all_to_all | solution.py:51
Sparse Core Ops, SparseCore 0:
  359.7 123.2 all-gather.1
